TPU v7x, 32 devices: a whole 2x2x4 slice. The times are simulated.
32 devices in a mesh: seq: 8 (over y, x, core), head: 4 (over z).
Axes of the slice: x: 2, y: 2, z: 4, core: 2. Of those that a mesh axis runs over, the one named last changes fastest.
Arguments:
- mid: bfloat16 [2048, 3072], P('seq'), may hold values from -20 to 20
- second_in: bfloat16 [2048, 3072], P('seq'), may hold values from -20 to 20
- cotangent: bfloat16 [2048, 3072], P('seq'), may hold values from -6 to 6
- w_key: bfloat16 [3072, 1024], P(None, 'head'), may hold values from -0.109375 to 0.109375
- w_value: bfloat16 [3072, 1024], P(None, 'head'), may hold values from -0.109375 to 0.109375
- w_query: bfloat16 [2, 3072, 3072], P(None, None, 'head'), may hold values from -0.109375 to 0.109375
- w_out: bfloat16 [2, 3072, 3072], P(None, 'head'), may hold values from -0.109375 to 0.109375
- w_ret_out: bfloat16 [3072, 3072], P('head'), may hold values from -0.109375 to 0.109375
- ret_query: bfloat16 [2048, 3072], P('seq', 'head'), may hold values from -6 to 6
- ret_key: bfloat16 [2048, 3072], P('seq', 'head'), may hold values from -3 to 3
- ret_value: bfloat16 [2048, 3072], P('seq', 'head'), may hold values from -6 to 6
- gate: float32 [24, 2048], P('head', 'seq'), may hold values from 0 to 6
- decay_exp: int32 [24], P('head'), may hold values from 0 to 256
- mask_start: int32 [16], P('seq'), may hold values from 0 to 1920, as said below
Outputs:
- grad_mid: bfloat16 [2048, 3072], P('seq')
- grad_ret_query: bfloat16 [2048, 3072], P('seq', 'head')
- grad_ret_key: bfloat16 [2048, 3072], P('seq', 'head')
- grad_ret_value: bfloat16 [2048, 3072], P('seq', 'head')
- grad_w_key: float32 [3072, 1024], P(None, 'head')
- grad_w_value: float32 [3072, 1024], P(None, 'head')
Inputs may be any that keep to these rules, and one draw needn't show every extreme that they name: `mask_start`: the entry of each block of 128 queries is at most the position of that block's first query.
All inputs are finite; a program needn't handle non-finite values.
Results may differ from a plain program's by a relative error of at most 0.025.
The roundings to bfloat16 on the way count: a program that leaves them out, or rounds other values in their place, can miss the bound.
Values may be sent and summed in bfloat16 or wider, within the bound.
A program may use at most 192 MiB of HBM per device.

v0:
```python
import functools
import math

import jax
import jax.numpy as jnp
from jax import lax
from jax.experimental import pallas as pl
from jax.experimental.pallas import tpu as pltpu
from jax.sharding import PartitionSpec as P

E = 128
BLK = 128
RC = 128
F32 = jnp.float32
BF16 = jnp.bfloat16


def contract_last(left, right):
    return lax.dot_general(left, right, (((1,), (1,)), ((), ())), preferred_element_type=F32)


def contract_first(left, right):
    return lax.dot_general(left, right, (((0,), (0,)), ((), ())), preferred_element_type=F32)


def send(src, dst, send_sem, recv_sem, axis, index):
    return pltpu.make_async_remote_copy(
        src_ref=src,
        dst_ref=dst,
        send_sem=send_sem,
        recv_sem=recv_sem,
        device_id={axis: index},
        device_id_type=pl.DeviceIdType.MESH,
    )


class SeqPlace:
    def __init__(self):
        self.peers = lax.axis_size("seq")
        self.chips = self.peers // 2
        self.me = lax.axis_index("seq")
        self.chip = self.me // 2
        self.core = lax.rem(self.me, 2)
        self.sibling = self.me + 1 - 2 * self.core

    def mate(self, k):
        return lax.rem(self.me + 2 * k, self.peers)

    def mate_of_sibling(self, k):
        return lax.rem(self.sibling + 2 * k, self.peers)


def rows_at(ref, index, rows):
    return ref.at[pl.ds(pl.multiple_of(index * rows, rows), rows)]


class Gather:
    def __init__(self, place, source, out, sems):
        self.place, self.source, self.out = place, source, out
        self.sends, self.forwards, self.arrivals = sems
        self.rows = out.shape[0] // place.peers

    @staticmethod
    def semaphores(peers):
        return [
            pltpu.SemaphoreType.DMA((peers // 2,)),
            pltpu.SemaphoreType.DMA((peers // 2,)),
            pltpu.SemaphoreType.DMA((peers,)),
        ]

    def chunk(self, index):
        return rows_at(self.out, index, self.rows)

    def direct(self, k):
        p = self.place
        return send(self.source, self.chunk(p.me), self.sends.at[k], self.arrivals.at[p.me], "seq", p.mate(k))

    def relayed(self, k):
        p = self.place
        at = p.mate(k)
        src = self.source if k == 0 else self.chunk(at)
        return send(src, self.chunk(at), self.forwards.at[k], self.arrivals.at[at], "seq", p.sibling)

    def arrival(self, index):
        p = self.place
        return send(self.source, self.chunk(index), self.sends.at[0], self.arrivals.at[index], "seq", p.sibling)

    def start(self):
        for k in range(1, self.place.chips):
            self.direct(k).start()
        self.relayed(0).start()

    def relay(self):
        for k in range(1, self.place.chips):
            self.arrival(self.place.mate(k)).wait_recv()
            self.relayed(k).start()

    def finish(self):
        p = self.place
        for k in range(p.chips):
            self.arrival(p.mate_of_sibling(k)).wait_recv()
        for k in range(1, p.chips):
            self.direct(k).wait_send()
        for k in range(p.chips):
            self.relayed(k).wait_send()


class Scatter:
    def __init__(self, place, source, scratch):
        self.place, self.source = place, source
        self.from_sibling, self.summed, self.landed = scratch[:3]
        self.pair_send, self.pair_recv, self.far_send, self.far_recv = scratch[3:]

    @staticmethod
    def scratch(peers, *chunk):
        chips = peers // 2
        return [pltpu.VMEM((chips, *chunk), BF16)] * 3 + [pltpu.SemaphoreType.DMA((chips,))] * 4

    def pair(self, i):
        p = self.place
        return send(
            self.source.at[2 * i + 1 - p.core],
            self.from_sibling.at[i],
            self.pair_send.at[i],
            self.pair_recv.at[i],
            "seq",
            p.sibling,
        )

    def far(self, k):
        p = self.place
        return send(
            self.summed.at[k], self.landed.at[k], self.far_send.at[k], self.far_recv.at[k], "seq", p.mate(k)
        )

    def pair_total(self, i):
        p = self.place
        self.pair(i).wait_recv()
        return self.source[2 * i + p.core].astype(F32) + self.from_sibling[i].astype(F32)

    def start(self):
        for k in range(self.place.chips):
            self.pair(lax.rem(self.place.chip + 1 + k, self.place.chips)).start()

    def combine(self):
        p = self.place
        for k in range(1, p.chips):
            self.summed[k] = self.pair_total(lax.rem(p.chip + k, p.chips)).astype(BF16)
            self.far(k).start()

    def total(self):
        p = self.place
        total = self.pair_total(p.chip)
        for k in range(1, p.chips):
            self.far(k).wait_recv()
            total = total + self.landed[k].astype(F32)
        return total

    def finish(self):
        for i in range(self.place.chips):
            self.pair(i).wait_send()
        for k in range(1, self.place.chips):
            self.far(k).wait_send()


SUB = 2
AHEAD = 3


class LineSum:
    def __init__(self, residual, total, scratch, produce, consume):
        self.residual, self.total = residual, total
        self.landed, self.summed, self.other = scratch[:3]
        self.in_send, self.in_recv, self.swap_recv, self.back_send, self.back_recv = scratch[3:]
        self.produce, self.consume = produce, consume
        self.count, self.rows, self.width = self.summed.shape
        self.n = lax.axis_size("head")
        self.z = lax.axis_index("head")
        low = self.z < self.n // 2
        self.depth = jnp.where(low, self.z, self.n - 1 - self.z)
        self.inward = jnp.where(low, self.z + 1, self.z - 1)
        self.outward = jnp.where(low, self.z - 1, self.z + 1)
        self.inner = self.depth == self.n // 2 - 1
        self.outer = self.depth == 0
        self.lag = self.n // 2 - self.depth + jnp.where(self.outer, AHEAD, 0)
        self.steps = self.count + self.lag

    @staticmethod
    def scratch(count, rows, width):
        sems = pltpu.SemaphoreType.DMA((count, SUB))
        return [pltpu.VMEM((count, rows, width), BF16)] * 3 + [sems] * 5

    def piece(self, j, s):
        size = self.rows // SUB
        return j, pl.ds(s * size, size)

    def up(self, j, s):
        at = self.piece(j, s)
        return send(
            self.summed.at[at], self.landed.at[at], self.in_send.at[j, s], self.in_recv.at[j, s],
            "head", self.inward,
        )

    def swap(self, j, s):
        at = self.piece(j, s)
        return send(
            self.summed.at[at], self.other.at[at], self.in_send.at[j, s], self.swap_recv.at[j, s],
            "head", self.inward,
        )

    def back(self, j, s):
        at = self.piece(j, s)
        return send(
            self.total.at[at], self.total.at[at], self.back_send.at[j, s], self.back_recv.at[j, s],
            "head", self.outward,
        )

    def reduce(self, j):
        part = self.produce(j)
        size = self.rows // SUB
        for s in range(SUB):
            at = self.piece(j, s)
            mine = part[s * size : (s + 1) * size]

            @pl.when(self.outer)
            def _(at=at, mine=mine):
                self.summed[at] = mine.astype(BF16)

            @pl.when(jnp.logical_not(self.outer))
            def _(at=at, mine=mine, s=s):
                self.up(j, s).wait_recv()
                self.summed[at] = (mine + self.landed[at].astype(F32)).astype(BF16)

            @pl.when(self.inner)
            def _(s=s):
                self.swap(j, s).start()

            @pl.when(jnp.logical_not(self.inner))
            def _(s=s):
                self.up(j, s).start()

    def finish_chunk(self, j):
        columns = pl.ds(pl.multiple_of(j * self.width, self.width), self.width)
        size = self.rows // SUB
        for s in range(SUB):
            at = self.piece(j, s)

            @pl.when(self.inner)
            def _(at=at, s=s):
                self.swap(j, s).wait_recv()
                both = self.summed[at].astype(F32) + self.other[at].astype(F32)
                if len(self.residual.shape) == 3:
                    rest = self.residual[at].astype(F32)
                else:
                    rest = self.residual[pl.ds(s * size, size), columns].astype(F32)
                self.total[at] = (rest + both).astype(BF16)

            @pl.when(jnp.logical_not(self.inner))
            def _(s=s):
                self.back(j, s).wait_recv()

            @pl.when(jnp.logical_not(self.outer))
            def _(s=s):
                self.back(j, s).start()

        self.consume(j)

    def run(self, first, last, beside=None):
        def step(t, carry):
            @pl.when(t < self.count)
            def _():
                self.reduce(t)

            @pl.when(t >= self.lag)
            def _():
                self.finish_chunk(t - self.lag)

            if beside is not None:
                beside(t)
            return carry

        lax.fori_loop(first, last, step, 0)

    def finish(self):
        def step(j, carry):
            for s in range(SUB):
                self.up(j, s).wait_send()

                @pl.when(jnp.logical_not(self.outer))
                def _(s=s):
                    self.back(j, s).wait_send()

            return carry

        lax.fori_loop(0, self.count, step, 0)


class Stream:
    def __init__(self, source, held, sem):
        self.source, self.held, self.sem = source, held, sem
        self.count = held.shape[0]

    def copy(self, i):
        return pltpu.make_async_copy(self.source(i), self.held.at[i], self.sem.at[i])

    def start(self):
        for i in range(self.count):
            self.copy(i).start()

    def wait(self, i):
        self.copy(i).wait()


def row_tiles(ref, layer, size):
    if layer is None:
        return lambda i: ref.at[pl.ds(pl.multiple_of(i * size, size), size), :]
    return lambda i: ref.at[layer, pl.ds(pl.multiple_of(i * size, size), size), :]


def column_tiles(ref, layer, size):
    if layer is None:
        return lambda i: ref.at[:, pl.ds(pl.multiple_of(i * size, size), size)]
    return lambda i: ref.at[layer, :, pl.ds(pl.multiple_of(i * size, size), size)]


def meet(seq, head):
    barrier = pltpu.get_barrier_semaphore()
    expected = 0

    def greet(axis, index):
        pl.semaphore_signal(
            barrier, inc=1, device_id={axis: index}, device_id_type=pl.DeviceIdType.MESH
        )

    if seq is not None:
        for k in range(1, seq.chips):
            greet("seq", seq.mate(k))
        greet("seq", seq.sibling)
        expected = seq.chips
    if head:
        n, z = lax.axis_size("head"), lax.axis_index("head")

        @pl.when(z > 0)
        def _():
            greet("head", z - 1)

        @pl.when(z < n - 1)
        def _():
            greet("head", z + 1)

        expected = expected + jnp.where(z > 0, 1, 0) + jnp.where(z < n - 1, 1, 0)
    pl.semaphore_wait(barrier, expected)


def call(kernel, name, number, outs, scratch, *operands, far=0, limit=56, near=0):
    whole = pl.BlockSpec(memory_space=pltpu.VMEM)
    return pl.pallas_call(
        kernel,
        out_shape=outs,
        in_specs=[pl.BlockSpec(memory_space=pltpu.SMEM)] * near
        + [whole] * (len(operands) - far - near)
        + [pl.BlockSpec(memory_space=pltpu.HBM)] * far,
        out_specs=jax.tree.map(lambda _: whole, outs),
        scratch_shapes=scratch,
        compiler_params=pltpu.CompilerParams(
            collective_id=number, has_side_effects=True, vmem_limit_bytes=limit * 2**20
        ),
        name=name,
    )(*operands)


def gather_kernel(x_ref, out_ref, *sems):
    place = SeqPlace()
    meet(place, False)
    gather = Gather(place, x_ref, out_ref, sems)
    gather.start()
    out_ref[pl.ds(pl.multiple_of(place.me * gather.rows, gather.rows), gather.rows), :] = x_ref[...]
    gather.relay()
    gather.finish()


def gather_seq(x, name, number):
    peers = lax.axis_size("seq")
    out = jax.ShapeDtypeStruct((peers * x.shape[0], x.shape[1]), x.dtype)
    return call(gather_kernel, name, number, out, Gather.semaphores(peers), x)


def tile_of(width):
    return 256 if width % 256 == 0 else E


def gather_project_kernel(
    second_far, cotangent_far, mid_far, wk_ref, wv_ref, wq_ref, wo_ref,
    out_ref, q1_ref, g1_ref, q0_ref,
    second_ref, cotangent_ref, mid_ref, kv_columns, columns, rows,
    input_sem, kv_sem, column_sem, row_sem, *sems
):
    place = SeqPlace()
    width = q1_ref.shape[1]
    tile = tile_of(width)
    pieces = width // tile
    half = out_ref.shape[1] // 2

    def kv_copy(i):
        return pltpu.make_async_copy((wk_ref, wv_ref)[i], kv_columns.at[i], kv_sem.at[i])

    def column_copy(layer, i):
        return pltpu.make_async_copy(
            wq_ref.at[layer, :, pl.ds(i * tile, tile)], columns.at[layer, i], column_sem.at[layer, i]
        )

    def row_copy(i):
        return pltpu.make_async_copy(wo_ref.at[1, pl.ds(i * tile, tile), :], rows.at[i], row_sem.at[i])

    def input_copy(i):
        source = (mid_far, second_far, cotangent_far)[i]
        return pltpu.make_async_copy(source, (mid_ref, second_ref, cotangent_ref)[i], input_sem.at[i])

    input_copy(0).start()
    for i in range(2):
        kv_copy(i).start()
    input_copy(1).start()
    for i in range(pieces):
        column_copy(1, i).start()
    input_copy(2).start()
    for i in range(pieces):
        row_copy(i).start()
    for i in range(pieces):
        column_copy(0, i).start()
    own = rows_at(out_ref, place.me, out_ref.shape[0] // place.peers)
    gather = Gather(place, own, out_ref, sems)
    input_copy(0).wait()
    for i in range(2):
        kv_copy(i).wait()
        own[:, i * half : (i + 1) * half] = jnp.dot(
            mid_ref[...], kv_columns[i], preferred_element_type=F32
        ).astype(BF16)
    meet(place, False)
    gather.start()
    input_copy(1).wait()
    for i in range(pieces):
        column_copy(1, i).wait()
        q1_ref[:, i * tile : (i + 1) * tile] = jnp.dot(
            second_ref[...], columns[1, i], preferred_element_type=F32
        ).astype(BF16)
    input_copy(2).wait()
    for i in range(pieces):
        row_copy(i).wait()
        g1_ref[:, i * tile : (i + 1) * tile] = contract_last(cotangent_ref[...], rows[i]).astype(BF16)
    for i in range(pieces):
        column_copy(0, i).wait()
        q0_ref[:, i * tile : (i + 1) * tile] = jnp.dot(
            mid_ref[...], columns[0, i], preferred_element_type=F32
        ).astype(BF16)
    gather.relay()
    gather.finish()


def gather_project(second_in, cotangent, mid, w_key, w_value, w_query, w_out):
    peers = lax.axis_size("seq")
    depth, width = w_query.shape[1:]
    tile = tile_of(width)
    pieces = width // tile
    half = w_key.shape[1]
    projected = jax.ShapeDtypeStruct((mid.shape[0], width), BF16)
    outs = (jax.ShapeDtypeStruct((peers * mid.shape[0], 2 * half), BF16),) + (projected,) * 3
    scratch = [
        pltpu.VMEM(second_in.shape, BF16),
        pltpu.VMEM(cotangent.shape, BF16),
        pltpu.VMEM(mid.shape, BF16),
        pltpu.VMEM((2, depth, half), BF16),
        pltpu.VMEM((2, pieces, depth, tile), BF16),
        pltpu.VMEM((pieces, tile, depth), BF16),
        pltpu.SemaphoreType.DMA((3,)),
        pltpu.SemaphoreType.DMA((2,)),
        pltpu.SemaphoreType.DMA((2, pieces)),
        pltpu.SemaphoreType.DMA((pieces,)),
    ] + Gather.semaphores(peers)
    return call(
        gather_project_kernel, "gather_kv", 0, outs, scratch,
        second_in, cotangent, mid, w_key, w_value, w_query, w_out, far=7, limit=52,
    )


class Retention:
    def __init__(self, decay):
        self.decay = decay
        self.count = decay.shape[1]

    def columns(self, h):
        return pl.ds(pl.multiple_of(h * E, E), E)

    def tile(self, ref, h, c):
        return ref[c * RC : (c + 1) * RC, self.columns(h)]

    def row(self, h, c):
        return self.decay[h, c : c + 1, :]

    def across(self, h, c):
        row = jnp.broadcast_to(self.row(h, c), (RC, RC))
        return row, jnp.transpose(row)

    def end(self, h, c):
        return self.row(h, c)[:, RC - 1 : RC]

    def weights(self, row, column):
        later = lax.broadcasted_iota(jnp.int32, (RC, RC), 0)
        lower = later >= lax.broadcasted_iota(jnp.int32, (RC, RC), 1)
        return jnp.where(lower, jnp.exp(jnp.where(lower, column - row, 0.0)), 0.0)


def running_sum(values):
    lane = lax.rem(lax.broadcasted_iota(jnp.int32, values.shape, 1), RC)
    shift = 1
    while shift < RC:
        values = values + jnp.where(lane >= shift, pltpu.roll(values, shift, 1), 0.0)
        shift *= 2
    return values


def first_sum_kernel(
    exponent, query_grad, residual, gate, ret_query, ret_key, ret_value, wq_ref, wo_ref,
    total, grad_out, accum, second, own_states, states, decays,
    logs, wq, wo, acc, wq_sem, wo_sem, *scratch
):
    place = SeqPlace()
    width = wq.shape[1]
    heads = second.shape[0]
    wq_tiles = Stream(row_tiles(wq_ref, 1, width), wq, wq_sem)
    wo_tiles = Stream(column_tiles(wo_ref, 0, width), wo, wo_sem)
    wq_tiles.start()
    wo_tiles.start()

    def produce(j):
        wq_tiles.wait(j)
        return contract_last(query_grad[...], wq[j])

    def consume(j):
        wo_tiles.wait(j)
        acc[...] += contract_last(total[j], wo[j])

    meet(place, True)
    line = LineSum(residual, total, scratch[:8], produce, consume)
    own_decay = rows_at(decays, place.me, decays.shape[0] // place.peers)
    own_state = rows_at(states, place.me, states.shape[0] // place.peers)
    small = Gather(place, own_decay, decays, scratch[8:11])
    large = Gather(place, own_state, states, scratch[11:14])
    acc[...] = jnp.zeros_like(acc)
    for h in range(heads):
        power = jnp.broadcast_to(-exponent[h].astype(F32) / 64.0, (1, gate.shape[1]))
        logs[h : h + 1, :] = -jnp.exp2(power) * gate[h : h + 1, :]
    sums = running_sum(logs[...])
    for h in range(heads):
        for c in range(accum.shape[1]):
            accum[h, c : c + 1, :] = sums[h : h + 1, c * RC : (c + 1) * RC]
    own_decay[...] = jnp.zeros_like(own_decay)
    ret = Retention(accum)

    def beside(h):
        @pl.when(h < heads)
        def _():
            state = jnp.zeros((E, E), F32)
            decay = jnp.zeros((1, 1), F32)
            for c in range(ret.count):
                row, column = ret.across(h, c)
                end = ret.end(h, c)
                key = ret.tile(ret_key, h, c)
                shrunk = (jnp.exp(end - column) * key.astype(F32)).astype(BF16)
                here = contract_first(shrunk, ret.tile(ret_value, h, c))
                own_states[h, c] = here
                state = jnp.exp(end) * state + here
                decay = decay + end
                products = contract_last(ret.tile(ret_query, h, c), key)
                second[h, c] = (ret.weights(row, column) * products).astype(BF16)
            states[pl.ds(pl.multiple_of((place.me * heads + h) * E, E), E), :] = state.astype(BF16)
            decays[pl.ds(place.me * own_decay.shape[0] + h, 1), :] = jnp.broadcast_to(decay, (1, E))

    line.run(0, heads, beside)
    small.start()
    large.start()
    line.run(heads, line.steps - 1)
    small.relay()
    large.relay()
    line.run(line.steps - 1, line.steps)
    grad_out[...] = acc[...].astype(BF16)
    small.finish()
    large.finish()
    line.finish()


def first_sum(decay_exp, query_grad, residual, gate, ret_query, ret_key, ret_value, w_query, w_out):
    peers = lax.axis_size("seq")
    rows, depth = residual.shape
    heads_width = query_grad.shape[1]
    out_width = w_out.shape[1]
    width = tile_of(depth)
    count = depth // width
    heads = ret_query.shape[1] // E
    blocks = rows // RC
    group = heads + -heads % 8
    outs = (
        jax.ShapeDtypeStruct((count, rows, width), BF16),
        jax.ShapeDtypeStruct((rows, out_width), BF16),
        jax.ShapeDtypeStruct((heads, blocks, RC), F32),
        jax.ShapeDtypeStruct((heads, blocks, RC, RC), BF16),
        jax.ShapeDtypeStruct((heads, blocks, E, E), F32),
        jax.ShapeDtypeStruct((peers * heads * E, E), BF16),
        jax.ShapeDtypeStruct((peers * group, E), F32),
    )
    scratch = [
        pltpu.VMEM((group, rows), F32),
        pltpu.VMEM((count, width, heads_width), BF16),
        pltpu.VMEM((count, out_width, width), BF16),
        pltpu.VMEM((rows, out_width), F32),
        pltpu.SemaphoreType.DMA((count,)),
        pltpu.SemaphoreType.DMA((count,)),
    ] + LineSum.scratch(count, rows, width) + Gather.semaphores(peers) + Gather.semaphores(peers)
    return call(
        first_sum_kernel, "first_sum", 1, outs, scratch,
        decay_exp, query_grad, residual, gate, ret_query, ret_key, ret_value, w_query, w_out,
        far=2, limit=22, near=1,
    )


def second_sum_kernel(
    kv_part, query_grad, residual, mid,
    accum, second, own_states, states, decays, ret_query, ret_key, ret_value,
    wq_ref, wk_ref, wv_ref, wo_ref,
    grad_mid, totals, grad_query, inner_key, inner_value, own_grads, grads,
    grad_o, entering, total, wq, wk, wv, wo, part, kv_grad, weights, acc,
    wq_sem, wk_sem, wv_sem, wo_sem, *scratch
):
    place = SeqPlace()
    count, rows, width = part.shape
    half = kv_grad.shape[1] // 2
    wq_tiles = Stream(row_tiles(wq_ref, 0, width), wq, wq_sem)
    wk_tiles = Stream(row_tiles(wk_ref, None, width), wk, wk_sem)
    wv_tiles = Stream(row_tiles(wv_ref, None, width), wv, wv_sem)
    wo_tiles = Stream(column_tiles(wo_ref, None, width), wo, wo_sem)
    for tiles in (wq_tiles, wk_tiles, wv_tiles, wo_tiles):
        tiles.start()

    def produce(j):
        wk_tiles.wait(j)
        wv_tiles.wait(j)
        return (
            part[j]
            + contract_last(kv_grad[:, :half], wk[j])
            + contract_last(kv_grad[:, half:], wv[j])
        )

    def consume(j):
        wo_tiles.wait(j)
        acc[...] += contract_last(total[j], wo[j])

    def lower(j, carry):
        wq_tiles.wait(j)
        part[j] = contract_last(query_grad[...], wq[j])
        return carry

    meet(place, True)
    scatter_kv = Scatter(place, kv_part, scratch[8:15])
    scatter_kv.start()
    lax.fori_loop(0, 2, lower, 0)
    scatter_kv.combine()
    lax.fori_loop(2, count, lower, 0)
    acc[...] = jnp.zeros_like(acc)
    across = scatter_kv.total()
    for side in (0, 1):
        kv_grad[:, side * half : (side + 1) * half] = jnp.transpose(across[side]).astype(BF16)
    line = LineSum(residual, total, scratch[:8], produce, consume)
    scatter = Scatter(place, weights, scratch[15:22])
    own = rows_at(totals, place.me, totals.shape[0] // place.peers)
    gather = Gather(place, own, totals, scratch[22:25])
    ends = Gather(place, rows_at(grads, place.me, grads.shape[0] // place.peers), grads, scratch[25:28])
    ret = Retention(accum)
    heads = second.shape[0]
    group = decays.shape[0] // place.peers

    def beside(t):
        h = t - late

        @pl.when((h >= 0) & (h < heads))
        def _():
            def hop(s, state):
                grown = jnp.exp(decays[pl.ds(s * group + h, 1), :]) * state
                return grown + states[pl.ds(pl.multiple_of((s * heads + h) * E, E), E), :].astype(F32)

            state = lax.fori_loop(0, place.me, hop, jnp.zeros((E, E), F32))
            for c in range(ret.count):
                entering[h, c] = state.astype(BF16)
                state = jnp.exp(ret.end(h, c)) * state + own_states[h, c]

    def own_grad(h, carry):
        state = jnp.zeros((E, E), F32)
        for c in reversed(range(ret.count)):
            row, column = ret.across(h, c)
            grown = (jnp.exp(column) * ret.tile(ret_query, h, c).astype(F32)).astype(BF16)
            here = contract_first(grown, ret.tile(grad_o, h, c)) * (1.0 / E)
            own_grads[h, c] = here
            state = here + jnp.exp(ret.end(h, c)) * state
        grads[pl.ds(pl.multiple_of((place.me * heads + h) * E, E), E), :] = state.astype(BF16)
        return carry

    def inner(h, carry):
        for c in range(ret.count):
            row, column = ret.across(h, c)
            rows_here = slice(c * RC, (c + 1) * RC)
            grad = ret.tile(grad_o, h, c)
            products = contract_last(grad, ret.tile(ret_value, h, c))
            first = (ret.weights(row, column) * products).astype(BF16)
            near = jnp.dot(first, ret.tile(ret_key, h, c), preferred_element_type=F32)
            carried = contract_last(grad, entering[h, c])
            grad_query[rows_here, ret.columns(h)] = (
                (near + jnp.exp(column) * carried) * (1.0 / E)
            ).astype(BF16)
            inner_key[rows_here, ret.columns(h)] = contract_first(first, ret.tile(ret_query, h, c)) * (1.0 / E)
            inner_value[rows_here, ret.columns(h)] = contract_first(second[h, c], grad) * (1.0 / E)
        return carry

    early = line.lag - 1
    late = line.steps - 1 - heads
    line.run(0, early)
    size = weights.shape[1]
    for i in range(place.peers):
        weights[i] = contract_first(mid[:, i * size : (i + 1) * size], kv_grad[...]).astype(BF16)
    scatter.start()
    line.run(early, early + 2)
    scatter.combine()
    line.run(early + 2, early + 9, beside)
    own[...] = scatter.total().astype(BF16)
    gather.start()
    line.run(early + 9, line.steps, beside)
    grad_o[...] = acc[...].astype(BF16)
    lax.fori_loop(0, heads, own_grad, 0)
    ends.start()
    for j in range(count):
        grad_mid[:, j * width : (j + 1) * width] = total[j]
    gather.relay()
    lax.fori_loop(0, heads, inner, 0)
    gather.finish()
    scatter.finish()
    ends.relay()
    ends.finish()
    scatter_kv.finish()
    line.finish()


def second_sum(kv_part, query_grad, residual, mid, kept, ret_query, ret_key, ret_value, w_query, w_key, w_value, w_ret_out):
    peers = lax.axis_size("seq")
    rows, depth = mid.shape
    heads_width = query_grad.shape[1]
    out_width = w_ret_out.shape[0]
    both = 2 * w_key.shape[1]
    width = tile_of(depth)
    count = depth // width
    outs = (
        jax.ShapeDtypeStruct((rows, depth), BF16),
        jax.ShapeDtypeStruct((depth, both), BF16),
        jax.ShapeDtypeStruct((rows, out_width), BF16),
        jax.ShapeDtypeStruct((rows, out_width), F32),
        jax.ShapeDtypeStruct((rows, out_width), F32),
        jax.ShapeDtypeStruct(kept[2].shape, F32),
        jax.ShapeDtypeStruct(kept[3].shape, BF16),
    )
    scratch = [
        pltpu.VMEM((rows, out_width), BF16),
        pltpu.VMEM(kept[2].shape, BF16),
        pltpu.VMEM((count, rows, width), BF16),
        pltpu.VMEM((count, width, heads_width), BF16),
        pltpu.VMEM((count, width, both // 2), BF16),
        pltpu.VMEM((count, width, both // 2), BF16),
        pltpu.VMEM((count, out_width, width), BF16),
        pltpu.VMEM((count, rows, width), F32),
        pltpu.VMEM((rows, both), BF16),
        pltpu.VMEM((peers, depth // peers, both), BF16),
        pltpu.VMEM((rows, out_width), F32),
    ] + [pltpu.SemaphoreType.DMA((count,))] * 4
    scratch += (
        LineSum.scratch(count, rows, width)
        + Scatter.scratch(peers, *kv_part.shape[1:])
        + Scatter.scratch(peers, depth // peers, both)
        + Gather.semaphores(peers)
        + Gather.semaphores(peers)
    )
    return call(
        second_sum_kernel, "second_sum", 3, outs, scratch,
        kv_part, query_grad, residual, mid, *kept, ret_query, ret_key, ret_value,
        w_query, w_key, w_value, w_ret_out, far=4, limit=41,
    )


def last_kernel(
    accum, decays, grads, own_grads, inner_key, inner_value, ret_key, ret_value, totals,
    grad_key, grad_value, grad_w_key, grad_w_value, wide, sems
):
    place = SeqPlace()
    ret = Retention(accum)
    heads = own_grads.shape[0]
    group = decays.shape[0] // place.peers
    pieces, size, half = wide.shape[1:]

    def copy(side, i):
        out = (grad_w_key, grad_w_value)[side]
        return pltpu.make_async_copy(wide.at[side, i], out.at[pl.ds(i * size, size)], sems.at[side, i])

    for i in range(pieces):
        for side in (0, 1):
            wide[side, i] = totals[i * size : (i + 1) * size, side * half : (side + 1) * half].astype(F32)
            copy(side, i).start()

    def head(h, carry):
        def hop(k, state):
            s = place.peers - 1 - k
            here = grads[pl.ds(pl.multiple_of((s * heads + h) * E, E), E), :].astype(F32)
            return here + jnp.exp(decays[pl.ds(s * group + h, 1), :]) * state

        state = lax.fori_loop(0, place.peers - 1 - place.me, hop, jnp.zeros((E, E), F32))
        for c in reversed(range(ret.count)):
            rows_here = slice(c * RC, (c + 1) * RC)
            row, column = ret.across(h, c)
            end = ret.end(h, c)
            after = state.astype(BF16)
            shrink = jnp.exp(end - column)
            at_key = contract_last(ret.tile(ret_value, h, c), after)
            at_value = jnp.dot(ret.tile(ret_key, h, c), after, preferred_element_type=F32)
            grad_key[rows_here, ret.columns(h)] = (
                inner_key[rows_here, ret.columns(h)] + shrink * at_key
            ).astype(BF16)
            grad_value[rows_here, ret.columns(h)] = (
                inner_value[rows_here, ret.columns(h)] + shrink * at_value
            ).astype(BF16)
            state = own_grads[h, c] + jnp.exp(end) * state
        return carry

    lax.fori_loop(0, heads, head, 0)
    for i in range(pieces):
        for side in (0, 1):
            copy(side, i).wait()


def last(accum, decays, grads, own_grads, inner_key, inner_value, ret_key, ret_value, totals):
    depth, both = totals.shape
    pieces = 6 if depth % (6 * E) == 0 else 1
    whole = pl.BlockSpec(memory_space=pltpu.VMEM)
    far = pl.BlockSpec(memory_space=pltpu.HBM)
    wide = jax.ShapeDtypeStruct((depth, both // 2), F32)
    narrow = jax.ShapeDtypeStruct(ret_key.shape, BF16)
    return pl.pallas_call(
        last_kernel,
        out_shape=(narrow, narrow, wide, wide),
        in_specs=[whole] * 9,
        out_specs=(whole, whole, far, far),
        scratch_shapes=[
            pltpu.VMEM((2, pieces, depth // pieces, both // 2), F32),
            pltpu.SemaphoreType.DMA((2, pieces)),
        ],
        compiler_params=pltpu.CompilerParams(vmem_limit_bytes=24 * 2**20),
        name="last",
    )(accum, decays, grads, own_grads, inner_key, inner_value, ret_key, ret_value, totals)


UNROLL = (4, 2, 1)


def sweep(first, last, body, carry):
    for width in UNROLL:
        many = jnp.maximum(last - first, 0) // width

        def several(i, carry, first=first, width=width):
            for k in range(width):
                carry = body(first + width * i + k, carry)
            return carry

        carry = lax.fori_loop(0, many, several, carry)
        first = first + width * many
    return carry


def attention_kernel(group, has_prev, mask_ref, *refs):
    if has_prev:
        q_all, g_all, kv_ref, prev_ref, dq_all, dkv_ref, s_ref, acc_all = refs
        acc_all[...] = prev_ref[...]
    else:
        q_all, g_all, kv_ref, dq_all, dkv_ref, s_ref = refs
        acc_all = dkv_ref
        acc_all[...] = jnp.zeros_like(acc_all)
    heads = acc_all.shape[2] // E
    blocks = q_all.shape[0] // BLK

    def tile(i, carry):
        h, b = i // blocks, lax.rem(i, blocks)
        at = pl.ds(pl.multiple_of(b * BLK, BLK), BLK)
        across = pl.ds(pl.multiple_of(h * group * E, E), group * E)
        here = pl.ds(pl.multiple_of(h * E, E), E)
        attention_tile(
            group, mask_ref, b, q_all.at[at, across], g_all.at[at, across], kv_ref.at[:, here],
            kv_ref.at[:, pl.ds(pl.multiple_of((heads + h) * E, E), E)],
            dq_all.at[at, across], acc_all.at[:, :, here], s_ref,
        )
        return carry

    lax.fori_loop(0, heads * blocks, tile, 0)
    if has_prev:
        dkv_ref[...] = acc_all[...].astype(BF16)


def attention_tile(group, mask_ref, block, q_ref, g_ref, k_ref, v_ref, dq_ref, acc, s_ref):
    step = acc.shape[3]
    factor = 1.0 / math.sqrt(E)
    power = factor * math.log2(math.e)
    first_row = lax.axis_index("seq") * step + block * BLK
    first_key = mask_ref[block]
    rows = group * BLK
    q = jnp.concatenate([q_ref[:, i * E : (i + 1) * E] for i in range(group)], axis=0)
    g = jnp.concatenate([g_ref[:, i * E : (i + 1) * E] for i in range(group)], axis=0)
    q_across, g_across = jnp.transpose(q), jnp.transpose(g)
    low = first_key // step
    high = (first_row + BLK + step - 1) // step

    def span(j):
        return pl.ds(pl.multiple_of(j * step, step), step)

    def fold(values, combine):
        total = values[:, :E]
        for i in range(1, step // E):
            total = combine(total, values[:, i * E : (i + 1) * E])
        return total

    def score(masked, j, top):
        scores = contract_last(q, k_ref[span(j), :])
        if masked:
            at = j * step + lax.broadcasted_iota(jnp.int32, (BLK, step), 1)
            query_position = first_row + lax.broadcasted_iota(jnp.int32, (BLK, step), 0)
            seen = (at >= first_key) & (at <= query_position)
            seen = jnp.concatenate([seen] * group, axis=0)
            scores = jnp.where(seen, scores, -jnp.inf)
        s_ref[:, span(j)] = scores
        return jnp.maximum(top, fold(scores, jnp.maximum))

    inside, outside = functools.partial(score, False), functools.partial(score, True)
    top = outside(low, jnp.full((rows, E), -jnp.inf, F32))
    top = sweep(low + 1, high - 1, inside, top)
    top = lax.fori_loop(jnp.maximum(low + 1, high - 1), high, outside, top)
    top = jnp.max(top, axis=-1, keepdims=True)

    def raise_(j, total):
        raised = jnp.exp2((s_ref[:, span(j)] - top) * power)
        s_ref[:, span(j)] = raised
        return total + fold(raised, jnp.add)

    total = sweep(low, high, raise_, jnp.zeros((rows, E), F32))
    scale = 1.0 / jnp.sum(total, axis=-1, keepdims=True)

    def output(j, out):
        probs = (s_ref[:, span(j)] * scale).astype(BF16)
        return out + jnp.dot(probs, v_ref[span(j), :], preferred_element_type=F32)

    out = sweep(low, high, output, jnp.zeros((rows, E), F32)).astype(BF16)
    delta = jnp.sum(g.astype(F32) * out.astype(F32), axis=-1, keepdims=True)

    def back(j, dq):
        probs = s_ref[:, span(j)] * scale
        dprobs = contract_last(g, v_ref[span(j), :])
        dscores = (probs * (dprobs - delta) * factor).astype(BF16)
        acc[j, 0] += jnp.dot(q_across, dscores, preferred_element_type=F32)
        acc[j, 1] += jnp.dot(g_across, probs.astype(BF16), preferred_element_type=F32)
        return dq + jnp.dot(dscores, k_ref[span(j), :], preferred_element_type=F32)

    dq = sweep(low, high, back, jnp.zeros((rows, E), F32)).astype(BF16)
    for i in range(group):
        dq_ref[:, i * E : (i + 1) * E] = dq[i * BLK : (i + 1) * BLK, :]


def attention(mask_start, queries, grad_out, kv, previous):
    row_count, width = queries.shape
    key_count, both = kv.shape
    heads = both // (2 * E)
    group = width // (heads * E)
    step = row_count
    count = key_count // step
    has_prev = previous is not None
    part = jax.ShapeDtypeStruct((count, 2, heads * E, step), BF16 if has_prev else F32)
    scratch = [pltpu.VMEM((group * BLK, key_count), F32)]
    if has_prev:
        scratch += [pltpu.VMEM(part.shape, F32)]
    whole = pl.BlockSpec(memory_space=pltpu.VMEM)
    return pl.pallas_call(
        functools.partial(attention_kernel, group, has_prev),
        out_shape=(jax.ShapeDtypeStruct((row_count, width), BF16), part),
        in_specs=[pl.BlockSpec(memory_space=pltpu.SMEM)] + [whole] * (4 if has_prev else 3),
        out_specs=(whole, whole),
        scratch_shapes=scratch,
        compiler_params=pltpu.CompilerParams(vmem_limit_bytes=20 * 2**20),
        cost_estimate=pl.CostEstimate(
            flops=10 * row_count * width * key_count, bytes_accessed=8 * 2**20, transcendentals=0
        ),
        name="attention_back",
    )(mask_start, queries, grad_out, kv, *(() if previous is None else (previous,)))


def local(
    mid,
    second_in,
    cotangent,
    w_key,
    w_value,
    w_query,
    w_out,
    w_ret_out,
    ret_query,
    ret_key,
    ret_value,
    gate,
    decay_exp,
    mask_start,
):
    kv, queries, grad_out, lower_queries = gather_project(
        second_in, cotangent, mid, w_key, w_value, w_query, w_out
    )

    query_grad, upper = attention(mask_start, queries, grad_out, kv, None)
    upstream, grad_out, *kept = first_sum(
        decay_exp, query_grad, cotangent, gate, ret_query, ret_key, ret_value, w_query, w_out
    )
    query_grad, kv_part = attention(mask_start, lower_queries, grad_out, kv, upper)
    grad_mid, totals, grad_query, inner_key, inner_value, own_grads, grads = second_sum(
        kv_part, query_grad, upstream, mid,
        kept, ret_query, ret_key, ret_value, w_query, w_key, w_value, w_ret_out,
    )
    grad_key, grad_value, grad_w_key, grad_w_value = last(
        kept[0], kept[4], grads, own_grads, inner_key, inner_value, ret_key, ret_value, totals
    )
    return (grad_mid, grad_query, grad_key, grad_value, grad_w_key, grad_w_value)


def solution(mesh):
    placed = (
        P("seq", None),
        P("seq", None),
        P("seq", None),
        P(None, "head"),
        P(None, "head"),
        P(None, None, "head"),
        P(None, "head", None),
        P("head", None),
        P("seq", "head"),
        P("seq", "head"),
        P("seq", "head"),
        P("head", "seq"),
        P("head"),
        P("seq"),
    )
    return jax.shard_map(
        local,
        mesh=mesh,
        in_specs=placed,
        out_specs=(
            P("seq", None),
            P("seq", "head"),
            P("seq", "head"),
            P("seq", "head"),
            P(None, "head"),
            P(None, "head"),
        ),
        check_vma=False,
    )
```

profile of v0, /device:TPU:0, one launch (start us, length us, event | category | flops | bytes accessed | tf_op | source)
XLA Modules:
  0.0 213.2 jit_solution(16070625236904043525)
XLA Ops:
  0.6 0.0 copy-start.16
  0.6 0.0 slice-start
  0.7 0.0 slice-start.1
  0.7 26.9 %gather_kv.1 = (bf16[2048,512]{1,0:T(8,128)(2,1)}, bf16[256,768]{1,0:T(8,128)(2,1)S(1)}, bf16[256,768]{1,0:T(8,128)(2,1)S(1)}, bf16[256,768]{1,0:T(8,128)(2,1)S(1)}) custom-call(bf16[256,3072]{1,0:T(8,128)(2,1)} %second_far.1, bf16[256,3072]{1,0:T(8,128)(2,1)} %residual.1, bf16[256,3072]{1,0:T(8,128)(2,1)} %mid.1, bf16[3072,256]{1,0:T(8,128)(2,1)} %wk_ref.3, ...), custom_call_target="tpu_custom_call" | custom-call | tf_op jit(solution)/shard_map/gather_kv/pallas_call | solution.py:357
  27.5 0.0 copy-done.16
  27.6 0.0 copy-start.14
  27.6 1.6 copy-done.14
  29.1 0.0 slice-start.2
  29.2 0.0 copy-start
  29.2 0.0 copy-start.1
  29.2 0.0 copy-start.3
  29.2 0.0 copy-start.4
  29.2 0.0 copy-start.9
  29.2 0.0 copy-start.12
  29.2 0.0 copy-start.13
  29.2 6.9 %attention_back.2 = (bf16[256,768]{1,0:T(8,128)(2,1)S(1)}, f32[8,2,256,256]{3,2,1,0:T(8,128)S(1)}) custom-call(s32[2]{0:T(128)S(1)} %copy-done.16, bf16[256,768]{1,0:T(8,128)(2,1)S(1)} %get-tuple-element.33.refs_0_, bf16[256,768]{1,0:T(8,128)(2,1)S(1)} %get-tuple-element.34.refs_1_, bf16[2048,512]{1,0:T(8,128)(2,1)S(1)} %copy-done.14), custom_call_target="tpu_custom_call" | custom-call | flops 4026531840 | bytes 8388608 | tf_op jit(solution)/shard_map/attention_back/pallas_call | solution.py:988
  36.1 0.0 slice-done
  36.1 0.0 slice-done.1
  36.1 0.0 slice-done.2
  36.2 0.0 copy-done
  36.2 0.0 copy-done.1
  36.2 0.0 copy-done.3
  36.2 0.0 copy-done.4
  36.2 0.0 copy-done.9
  36.2 0.0 copy-done.12
  36.2 0.0 copy-done.13
  36.2 0.0 copy-start.15
  36.2 65.3 %first_sum.1 = (bf16[12,256,256]{2,1,0:T(8,128)(2,1)S(1)}, bf16[256,768]{1,0:T(8,128)(2,1)S(1)}, f32[6,2,128]{2,1,0:T(2,128)S(1)}, bf16[6,2,128,128]{3,2,1,0:T(8...) custom-call(s32[6]{0:T(128)S(1)} %copy-done.13, ...), custom_call_target="tpu_custom_call" | custom-call | tf_op jit(solution)/shard_map/first_sum/pallas_call | solution.py:357
  101.6 0.0 copy-start.7
  101.6 0.0 copy-start.10
  101.6 0.0 copy-done.15
  101.6 0.0 copy-start.2
  101.6 7.1 %attention_back.3 = (bf16[256,768]{1,0:T(8,128)(2,1)S(1)}, bf16[8,2,256,256]{3,2,1,0:T(8,128)(2,1)S(1)}) custom-call(s32[2]{0:T(128)S(1)} %copy-done.16, bf16[256,768]{1,0:T(8,128)(2,1)S(1)} %get-tuple-element.32.refs_0_, bf16[256,768]{1,0:T(8,128)(2,1)S(1)} %get-tuple-element.37.refs_1_, bf16[2048,512]{1,0:T(8,128)(2,1)S(1)} %copy-done.15, ...), custom_call_target="tpu_custom_call" | custom-call | flops 4026531840 | bytes 8388608 | tf_op jit(solution)/shard_map/attention_back/pallas_call | solution.py:988
  108.7 0.0 copy-done.7
  108.7 0.0 copy-done.10
  108.7 0.0 copy-start.6
  108.7 1.3 copy-done.6
  110.0 0.0 copy-done.2
  110.0 0.0 copy-start.8
  110.0 1.4 copy-done.8
  111.4 0.0 copy-start.11
  111.5 1.1 copy-done.11
  112.6 93.0 %second_sum.1 = (bf16[256,3072]{1,0:T(8,128)(2,1)S(1)}, bf16[3072,512]{1,0:T(8,128)(2,1)}, bf16[256,768]{1,0:T(8,128)(2,1)S(1)}, f32[256,768]{1,0:T(8,128)S(1)},...) custom-call(bf16[8,2,256,256]{3,2,1,0:T(8,128)(2,1)} %copy-done.6, ...), custom_call_target="tpu_custom_call" | custom-call | tf_op jit(solution)/shard_map/second_sum/pallas_call | solution.py:357
  205.6 0.0 copy-start.5
  205.6 1.9 copy-done.5
  207.5 3.8 %last.1 = (bf16[256,768]{1,0:T(8,128)(2,1)}, bf16[256,768]{1,0:T(8,128)(2,1)}, f32[3072,256]{1,0:T(8,128)}, f32[3072,256]{1,0:T(8,128)}) custom-call(f32[6,2,128]{2,1,0:T(2,128)S(1)} %get-tuple-element.42.accum, f32[64,128]{1,0:T(8,128)S(1)} %get-tuple-element.46.decays, bf16[6144,128]{1,0:T(8,128)(2,1)S(1)} %get-tuple-element.49.grads, ...), custom_call_target="tpu_custom_call" | custom-call | tf_op jit(solution)/shard_map/last/pallas_call | solution.py:849
  211.3 1.1 copy.22
  212.5 0.7 copy.23
  (1 shorter events, 0.0 us)
Async XLA Ops:
  0.6 26.9 %copy-start.16 = (s32[2]{0:T(128)S(1)}, s32[2]{0:T(128)}, u32[]{:S(2)}) copy-start(s32[2]{0:T(128)} %mask_ref.3) | copy-start | bytes 28
  0.6 35.5 %slice-start = ((s8[9437184]{0:T(1024)(128)(4,1)}), s8[4194304]{0:T(1024)(128)(4,1)S(1)}, s32[]{:S(2)}) async-start(s8[9437184]{0:T(1024)(128)(4,1)} %bitcast), calls=%async_computation | async-start | bytes 8388608
  0.7 35.5 %slice-start.1 = ((s8[9437184]{0:T(1024)(128)(4,1)}), s8[4194304]{0:T(1024)(128)(4,1)S(1)}, s32[]{:S(2)}) async-start(s8[9437184]{0:T(1024)(128)(4,1)} %bitcast), calls=%async_computation.1 | async-start | bytes 8388608
  27.6 1.6 copy-start.14
  29.1 7.0 %slice-start.2 = ((s8[9437184]{0:T(1024)(128)(4,1)}), s8[1048576]{0:T(1024)(128)(4,1)S(1)}, s32[]{:S(2)}) async-start(s8[9437184]{0:T(1024)(128)(4,1)} %bitcast), calls=%async_computation.2 | async-start | bytes 2097152
  29.2 7.0 %copy-start = (bf16[2,768,3072]{2,1,0:T(8,128)(2,1)S(1)}, bf16[2,768,3072]{2,1,0:T(8,128)(2,1)}, u32[]{:S(2)}) copy-start(bf16[2,768,3072]{2,1,0:T(8,128)(2,1)} %wo_ref.4) | copy-start | bytes 28311556
  29.2 7.0 %copy-start.1 = (bf16[256,3072]{1,0:T(8,128)(2,1)S(1)}, bf16[256,3072]{1,0:T(8,128)(2,1)}, u32[]{:S(2)}) copy-start(bf16[256,3072]{1,0:T(8,128)(2,1)} %residual.1) | copy-start | bytes 4718596
  29.2 7.0 %copy-start.3 = (bf16[256,768]{1,0:T(8,128)(2,1)S(1)}, bf16[256,768]{1,0:T(8,128)(2,1)}, u32[]{:S(2)}) copy-start(bf16[256,768]{1,0:T(8,128)(2,1)} %ret_key.5) | copy-start | bytes 1179652
  29.2 7.0 %copy-start.4 = (bf16[256,768]{1,0:T(8,128)(2,1)S(1)}, bf16[256,768]{1,0:T(8,128)(2,1)}, u32[]{:S(2)}) copy-start(bf16[256,768]{1,0:T(8,128)(2,1)} %ret_value.5) | copy-start | bytes 1179652
  29.2 7.0 %copy-start.9 = (bf16[256,768]{1,0:T(8,128)(2,1)S(1)}, bf16[256,768]{1,0:T(8,128)(2,1)}, u32[]{:S(2)}) copy-start(bf16[256,768]{1,0:T(8,128)(2,1)} %ret_query.3) | copy-start | bytes 1179652
  29.2 7.0 %copy-start.12 = (f32[6,256]{1,0:T(8,128)S(1)}, f32[6,256]{1,0:T(8,128)}, u32[]{:S(2)}) copy-start(f32[6,256]{1,0:T(8,128)} %gate.1) | copy-start | bytes 18436
  29.2 7.0 %copy-start.13 = (s32[6]{0:T(128)S(1)}, s32[6]{0:T(128)}, u32[]{:S(2)}) copy-start(s32[6]{0:T(128)} %exponent.1) | copy-start | bytes 76
  36.2 65.4 %copy-start.15 = (bf16[2048,512]{1,0:T(8,128)(2,1)S(1)}, bf16[2048,512]{1,0:T(8,128)(2,1)}, u32[]{:S(2)}) copy-start(bf16[2048,512]{1,0:T(8,128)(2,1)} %get-tuple-element.35.refs_2_) | copy-start | bytes 6291460
  101.6 7.1 %copy-start.7 = (bf16[6144,128]{1,0:T(8,128)(2,1)}, bf16[6144,128]{1,0:T(8,128)(2,1)S(1)}, u32[]{:S(2)}) copy-start(bf16[6144,128]{1,0:T(8,128)(2,1)S(1)} %get-tuple-element.45.states) | copy-start | bytes 4718596
  101.6 7.1 %copy-start.10 = (f32[6,2,128,128]{3,2,1,0:T(8,128)}, f32[6,2,128,128]{3,2,1,0:T(8,128)S(1)}, u32[]{:S(2)}) copy-start(f32[6,2,128,128]{3,2,1,0:T(8,128)S(1)} %get-tuple-element.44.own_states) | copy-start | bytes 2359300
  101.6 8.4 %copy-start.2 = (bf16[256,3072]{1,0:T(8,128)(2,1)S(1)}, bf16[256,3072]{1,0:T(8,128)(2,1)}, u32[]{:S(2)}) copy-start(bf16[256,3072]{1,0:T(8,128)(2,1)} %mid.1) | copy-start | bytes 4718596
  108.7 1.3 copy-start.6
  110.0 1.4 copy-start.8
  111.4 1.1 copy-start.11
  205.6 1.9 copy-start.5
where the time goes:
time: 214 us; the launch traced here: 213 us
  Pallas kernels  203 us (95%)
  local copies, waits for them, and re-layouts  9.29 us (4%)
    pallas_call x3, Pallas kernels, call(): pl.pallas_call(kernel, out_shape=outs, in_specs=[pl.BlockSpec(memory_spac...  185 us
    pallas_call x2, Pallas kernels, attention(): pl.pallas_call(functools.partial(attention_kernel, group, has_prev), out_...  14 us
    unnamed x42, local copies, waits for them, and re-layouts  9.29 us

commit v1 on v0

--- a/solution.py
+++ b/solution.py
@@ -170,8 +170,8 @@
 class LineSum:
     def __init__(self, residual, total, scratch, produce, consume):
         self.residual, self.total = residual, total
-        self.landed, self.summed, self.other = scratch[:3]
-        self.in_send, self.in_recv, self.swap_recv, self.back_send, self.back_recv = scratch[3:]
+        self.landed, self.summed = scratch[:2]
+        self.in_send, self.in_recv, self.swap_recv, self.back_send, self.back_recv = scratch[2:]
         self.produce, self.consume = produce, consume
         self.count, self.rows, self.width = self.summed.shape
         self.n = lax.axis_size("head")
@@ -188,7 +188,7 @@
     @staticmethod
     def scratch(count, rows, width):
         sems = pltpu.SemaphoreType.DMA((count, SUB))
-        return [pltpu.VMEM((count, rows, width), BF16)] * 3 + [sems] * 5
+        return [pltpu.VMEM((count, rows, width), BF16)] * 2 + [sems] * 5
 
     def piece(self, j, s):
         size = self.rows // SUB
@@ -204,7 +204,7 @@
     def swap(self, j, s):
         at = self.piece(j, s)
         return send(
-            self.summed.at[at], self.other.at[at], self.in_send.at[j, s], self.swap_recv.at[j, s],
+            self.summed.at[at], self.total.at[at], self.in_send.at[j, s], self.swap_recv.at[j, s],
             "head", self.inward,
         )
 
@@ -248,7 +248,7 @@
             @pl.when(self.inner)
             def _(at=at, s=s):
                 self.swap(j, s).wait_recv()
-                both = self.summed[at].astype(F32) + self.other[at].astype(F32)
+                both = self.summed[at].astype(F32) + self.total[at].astype(F32)
                 if len(self.residual.shape) == 3:
                     rest = self.residual[at].astype(F32)
                 else:
@@ -540,11 +540,11 @@
         acc[...] += contract_last(total[j], wo[j])
 
     meet(place, True)
-    line = LineSum(residual, total, scratch[:8], produce, consume)
+    line = LineSum(residual, total, scratch[:7], produce, consume)
     own_decay = rows_at(decays, place.me, decays.shape[0] // place.peers)
     own_state = rows_at(states, place.me, states.shape[0] // place.peers)
-    small = Gather(place, own_decay, decays, scratch[8:11])
-    large = Gather(place, own_state, states, scratch[11:14])
+    small = Gather(place, own_decay, decays, scratch[7:10])
+    large = Gather(place, own_state, states, scratch[10:13])
     acc[...] = jnp.zeros_like(acc)
     for h in range(heads):
         power = jnp.broadcast_to(-exponent[h].astype(F32) / 64.0, (1, gate.shape[1]))
@@ -659,7 +659,7 @@
         return carry
 
     meet(place, True)
-    scatter_kv = Scatter(place, kv_part, scratch[8:15])
+    scatter_kv = Scatter(place, kv_part, scratch[7:14])
     scatter_kv.start()
     lax.fori_loop(0, 2, lower, 0)
     scatter_kv.combine()
@@ -668,11 +668,11 @@
     across = scatter_kv.total()
     for side in (0, 1):
         kv_grad[:, side * half : (side + 1) * half] = jnp.transpose(across[side]).astype(BF16)
-    line = LineSum(residual, total, scratch[:8], produce, consume)
-    scatter = Scatter(place, weights, scratch[15:22])
+    line = LineSum(residual, total, scratch[:7], produce, consume)
+    scatter = Scatter(place, weights, scratch[14:21])
     own = rows_at(totals, place.me, totals.shape[0] // place.peers)
-    gather = Gather(place, own, totals, scratch[22:25])
-    ends = Gather(place, rows_at(grads, place.me, grads.shape[0] // place.peers), grads, scratch[25:28])
+    gather = Gather(place, own, totals, scratch[21:24])
+    ends = Gather(place, rows_at(grads, place.me, grads.shape[0] // place.peers), grads, scratch[24:27])
     ret = Retention(accum)
     heads = second.shape[0]
     group = decays.shape[0] // place.peers
@@ -786,7 +786,7 @@
     return call(
         second_sum_kernel, "second_sum", 3, outs, scratch,
         kv_part, query_grad, residual, mid, *kept, ret_query, ret_key, ret_value,
-        w_query, w_key, w_value, w_ret_out, far=4, limit=41,
+        w_query, w_key, w_value, w_ret_out, far=4, limit=39,
     )
 
 
@@ -991,7 +991,7 @@
         in_specs=[pl.BlockSpec(memory_space=pltpu.SMEM)] + [whole] * (4 if has_prev else 3),
         out_specs=(whole, whole),
         scratch_shapes=scratch,
-        compiler_params=pltpu.CompilerParams(vmem_limit_bytes=20 * 2**20),
+        compiler_params=pltpu.CompilerParams(vmem_limit_bytes=12 * 2**20),
         cost_estimate=pl.CostEstimate(
             flops=10 * row_count * width * key_count, bytes_accessed=8 * 2**20, transcendentals=0
         ),

time: 214 us -> 207 us (0.967)
  Pallas kernels: 203 us -> 197 us
    pallas_call x3, Pallas kernels: 185 us -> 180 us  [call(): pl.pallas_call(kernel, out_shape=outs, in_specs=[pl.BlockSpec(memory_spac...]
    unnamed x42 -> x44, local copies, waits for them, and re-layouts: 9.29 us -> 9.29 us
where the time goes in v1:
time: 207 us; the launch traced here: 208 us
  Pallas kernels  197 us (95%)
  local copies, waits for them, and re-layouts  9.29 us (4%)
    pallas_call x3, Pallas kernels, call(): pl.pallas_call(kernel, out_shape=outs, in_specs=[pl.BlockSpec(memory_spac...  180 us
    pallas_call x2, Pallas kernels, attention(): pl.pallas_call(functools.partial(attention_kernel, group, has_prev), out_...  14 us
    unnamed x44, local copies, waits for them, and re-layouts  9.29 us

profile of v1, /device:TPU:0, one launch (start us, length us, event | category | flops | bytes accessed | tf_op | source)
XLA Modules:
  0.0 207.7 jit_solution(13321028562181095315)
XLA Ops:
  0.6 0.0 copy-start.17
  0.6 0.0 slice-start
  0.7 0.0 slice-start.1
  0.7 26.9 %gather_kv.1 = (bf16[2048,512]{1,0:T(8,128)(2,1)}, bf16[256,768]{1,0:T(8,128)(2,1)S(1)}, bf16[256,768]{1,0:T(8,128)(2,1)S(1)}, bf16[256,768]{1,0:T(8,128)(2,1)S(1)}) custom-call(bf16[256,3072]{1,0:T(8,128)(2,1)} %second_far.1, bf16[256,3072]{1,0:T(8,128)(2,1)} %residual.1, bf16[256,3072]{1,0:T(8,128)(2,1)} %mid.1, bf16[3072,256]{1,0:T(8,128)(2,1)} %wk_ref.3, ...), custom_call_target="tpu_custom_call" | custom-call | tf_op jit(solution)/shard_map/gather_kv/pallas_call | solution.py:357
  27.5 0.0 copy-done.17
  27.6 0.0 copy-start.15
  27.6 1.6 copy-done.15
  29.1 0.0 slice-start.2
  29.1 0.0 copy-start
  29.1 0.0 copy-start.1
  29.1 0.0 copy-start.4
  29.2 0.0 copy-start.5
  29.2 0.0 copy-start.12
  29.2 0.0 copy-start.13
  29.2 0.0 copy-start.14
  29.2 6.9 %attention_back.2 = (bf16[256,768]{1,0:T(8,128)(2,1)S(1)}, f32[8,2,256,256]{3,2,1,0:T(8,128)S(1)}) custom-call(s32[2]{0:T(128)S(1)} %copy-done.17, bf16[256,768]{1,0:T(8,128)(2,1)S(1)} %get-tuple-element.33.refs_0_, bf16[256,768]{1,0:T(8,128)(2,1)S(1)} %get-tuple-element.34.refs_1_, bf16[2048,512]{1,0:T(8,128)(2,1)S(1)} %copy-done.15), custom_call_target="tpu_custom_call" | custom-call | flops 4026531840 | bytes 8388608 | tf_op jit(solution)/shard_map/attention_back/pallas_call | solution.py:988
  36.1 0.0 slice-done
  36.1 0.0 slice-done.1
  36.1 0.0 slice-done.2
  36.1 0.0 copy-done
  36.2 0.0 copy-done.1
  36.2 0.0 copy-done.4
  36.2 0.0 copy-done.5
  36.2 0.0 copy-done.12
  36.2 0.0 copy-done.13
  36.2 0.0 copy-done.14
  36.2 0.0 copy-start.16
  36.2 58.9 %first_sum.1 = (bf16[12,256,256]{2,1,0:T(8,128)(2,1)S(1)}, bf16[256,768]{1,0:T(8,128)(2,1)S(1)}, f32[6,2,128]{2,1,0:T(2,128)S(1)}, bf16[6,2,128,128]{3,2,1,0:T(8...) custom-call(s32[6]{0:T(128)S(1)} %copy-done.14, ...), custom_call_target="tpu_custom_call" | custom-call | tf_op jit(solution)/shard_map/first_sum/pallas_call | solution.py:357
  95.2 0.0 copy-start.8
  95.2 1.1 copy-done.8
  96.3 0.0 copy-start.10
  96.3 0.0 copy-done.16
  96.3 0.0 copy-start.2
  96.3 0.0 copy-start.3
  96.3 0.0 copy-start.9
  96.3 7.1 %attention_back.3 = (bf16[256,768]{1,0:T(8,128)(2,1)S(1)}, bf16[8,2,256,256]{3,2,1,0:T(8,128)(2,1)S(1)}) custom-call(s32[2]{0:T(128)S(1)} %copy-done.17, bf16[256,768]{1,0:T(8,128)(2,1)S(1)} %get-tuple-element.32.refs_0_, bf16[256,768]{1,0:T(8,128)(2,1)S(1)} %get-tuple-element.37.refs_1_, bf16[2048,512]{1,0:T(8,128)(2,1)S(1)} %copy-done.16, ...), custom_call_target="tpu_custom_call" | custom-call | flops 4026531840 | bytes 8388608 | tf_op jit(solution)/shard_map/attention_back/pallas_call | solution.py:988
  103.5 0.0 copy-done.10
  103.5 0.0 copy-start.7
  103.5 1.3 copy-done.7
  104.8 0.0 copy-done.2
  104.8 0.0 copy-done.3
  104.8 0.0 copy-done.9
  104.8 0.0 copy-start.11
  104.8 1.4 copy-done.11
  106.2 93.8 %second_sum.1 = (bf16[256,3072]{1,0:T(8,128)(2,1)S(1)}, bf16[3072,512]{1,0:T(8,128)(2,1)}, bf16[256,768]{1,0:T(8,128)(2,1)S(1)}, f32[256,768]{1,0:T(8,128)S(1)},...) custom-call(bf16[8,2,256,256]{3,2,1,0:T(8,128)(2,1)} %copy-done.7, ...), custom_call_target="tpu_custom_call" | custom-call | tf_op jit(solution)/shard_map/second_sum/pallas_call | solution.py:357
  200.0 0.0 copy-start.6
  200.0 1.9 copy-done.6
  201.9 3.8 %last.1 = (bf16[256,768]{1,0:T(8,128)(2,1)}, bf16[256,768]{1,0:T(8,128)(2,1)}, f32[3072,256]{1,0:T(8,128)}, f32[3072,256]{1,0:T(8,128)}) custom-call(f32[6,2,128]{2,1,0:T(2,128)S(1)} %get-tuple-element.42.accum, f32[64,128]{1,0:T(8,128)S(1)} %get-tuple-element.46.decays, bf16[6144,128]{1,0:T(8,128)(2,1)S(1)} %get-tuple-element.49.grads, ...), custom_call_target="tpu_custom_call" | custom-call | tf_op jit(solution)/shard_map/last/pallas_call | solution.py:849
  205.8 1.1 copy.22
  206.9 0.7 copy.23
  (1 shorter events, 0.0 us)
Async XLA Ops:
  0.6 26.9 %copy-start.17 = (s32[2]{0:T(128)S(1)}, s32[2]{0:T(128)}, u32[]{:S(2)}) copy-start(s32[2]{0:T(128)} %mask_ref.3) | copy-start | bytes 28
  0.6 35.5 %slice-start = ((s8[9437184]{0:T(1024)(128)(4,1)}), s8[4194304]{0:T(1024)(128)(4,1)S(1)}, s32[]{:S(2)}) async-start(s8[9437184]{0:T(1024)(128)(4,1)} %bitcast), calls=%async_computation | async-start | bytes 8388608
  0.7 35.5 %slice-start.1 = ((s8[9437184]{0:T(1024)(128)(4,1)}), s8[4194304]{0:T(1024)(128)(4,1)S(1)}, s32[]{:S(2)}) async-start(s8[9437184]{0:T(1024)(128)(4,1)} %bitcast), calls=%async_computation.1 | async-start | bytes 8388608
  27.6 1.6 copy-start.15
  29.1 7.0 %slice-start.2 = ((s8[9437184]{0:T(1024)(128)(4,1)}), s8[1048576]{0:T(1024)(128)(4,1)S(1)}, s32[]{:S(2)}) async-start(s8[9437184]{0:T(1024)(128)(4,1)} %bitcast), calls=%async_computation.2 | async-start | bytes 2097152
  29.1 7.0 %copy-start = (bf16[2,768,3072]{2,1,0:T(8,128)(2,1)S(1)}, bf16[2,768,3072]{2,1,0:T(8,128)(2,1)}, u32[]{:S(2)}) copy-start(bf16[2,768,3072]{2,1,0:T(8,128)(2,1)} %wo_ref.4) | copy-start | bytes 28311556
  29.1 7.0 %copy-start.1 = (bf16[256,3072]{1,0:T(8,128)(2,1)S(1)}, bf16[256,3072]{1,0:T(8,128)(2,1)}, u32[]{:S(2)}) copy-start(bf16[256,3072]{1,0:T(8,128)(2,1)} %residual.1) | copy-start | bytes 4718596
  29.1 7.0 %copy-start.4 = (bf16[256,768]{1,0:T(8,128)(2,1)S(1)}, bf16[256,768]{1,0:T(8,128)(2,1)}, u32[]{:S(2)}) copy-start(bf16[256,768]{1,0:T(8,128)(2,1)} %ret_key.5) | copy-start | bytes 1179652
  29.2 7.0 %copy-start.5 = (bf16[256,768]{1,0:T(8,128)(2,1)S(1)}, bf16[256,768]{1,0:T(8,128)(2,1)}, u32[]{:S(2)}) copy-start(bf16[256,768]{1,0:T(8,128)(2,1)} %ret_value.5) | copy-start | bytes 1179652
  29.2 7.0 %copy-start.12 = (bf16[256,768]{1,0:T(8,128)(2,1)S(1)}, bf16[256,768]{1,0:T(8,128)(2,1)}, u32[]{:S(2)}) copy-start(bf16[256,768]{1,0:T(8,128)(2,1)} %ret_query.3) | copy-start | bytes 1179652
  29.2 7.0 %copy-start.13 = (f32[6,256]{1,0:T(8,128)S(1)}, f32[6,256]{1,0:T(8,128)}, u32[]{:S(2)}) copy-start(f32[6,256]{1,0:T(8,128)} %gate.1) | copy-start | bytes 18436
  29.2 7.0 %copy-start.14 = (s32[6]{0:T(128)S(1)}, s32[6]{0:T(128)}, u32[]{:S(2)}) copy-start(s32[6]{0:T(128)} %exponent.1) | copy-start | bytes 76
  36.2 60.1 %copy-start.16 = (bf16[2048,512]{1,0:T(8,128)(2,1)S(1)}, bf16[2048,512]{1,0:T(8,128)(2,1)}, u32[]{:S(2)}) copy-start(bf16[2048,512]{1,0:T(8,128)(2,1)} %get-tuple-element.35.refs_2_) | copy-start | bytes 6291460
  95.2 1.1 copy-start.8
  96.3 7.1 %copy-start.10 = (bf16[6144,128]{1,0:T(8,128)(2,1)}, bf16[6144,128]{1,0:T(8,128)(2,1)S(1)}, u32[]{:S(2)}) copy-start(bf16[6144,128]{1,0:T(8,128)(2,1)S(1)} %get-tuple-element.45.states) | copy-start | bytes 4718596
  96.3 8.5 %copy-start.2 = (bf16[256,3072]{1,0:T(8,128)(2,1)S(1)}, bf16[256,3072]{1,0:T(8,128)(2,1)}, u32[]{:S(2)}) copy-start(bf16[256,3072]{1,0:T(8,128)(2,1)} %mid.1) | copy-start | bytes 4718596
  96.3 8.5 %copy-start.3 = (bf16[3072,256]{1,0:T(8,128)(2,1)S(1)}, bf16[3072,256]{1,0:T(8,128)(2,1)}, u32[]{:S(2)}) copy-start(bf16[3072,256]{1,0:T(8,128)(2,1)} %wk_ref.3) | copy-start | bytes 4718596
  96.3 8.5 %copy-start.9 = (bf16[12,256,256]{2,1,0:T(8,128)(2,1)S(1)}, bf16[12,256,256]{2,1,0:T(8,128)(2,1)}, u32[]{:S(2)}) copy-start(bf16[12,256,256]{2,1,0:T(8,128)(2,1)} %copy-done.8) | copy-start | bytes 4718596
  103.5 1.3 copy-start.7
  104.8 1.4 copy-start.11
  200.0 1.9 copy-start.6
